TPU v7x, 32 devices: a whole 2x2x4 slice. The times are simulated.
32 devices in a mesh: groups: 2 (over x), gx: 16 (over z, y, core).
Axes of the slice: x: 2, y: 2, z: 4, core: 2. Of those that a mesh axis runs over, the one named last changes fastest.
Arguments:
- wave_one: float32 [2, 512, 2048], P(None, 'groups', 'gx'), parts along dimension 1, may hold values from -6 to 6
- wave_two: float32 [2, 512, 2048], P(None, 'groups', 'gx'), parts along dimension 1, may hold values from -4.2 to 4.2
- mismatch: float32 [512, 2048], P('groups', 'gx'), parts along dimension 0, may hold values from -1.2 to 1.2
- plate: int32 [16, 64], P('groups', 'gx'), parts along dimension 0, may hold values from 0 to 15
- spot_low: int32 [1024], P('groups'), parts along dimension 0, may hold values from 64 to 255
- spot_high: int32 [1024], P('groups'), parts along dimension 0, may hold values from 256 to 447
- row_gain: float32 [1024], P('groups'), parts along dimension 0, may hold values from 0.5 to 3
- column_gain: float32 [1024], P('groups'), parts along dimension 0, may hold values from 0.5 to 3
Outputs:
- third: float32 [2, 512, 2048], P(None, 'groups', 'gx'), parts along dimension 1
- far_field: float32 [2, 1024, 512], P(None, ('groups', 'gx')), parts along dimension 1
- back_field: float32 [2, 512, 2048], P(None, 'groups', 'gx'), parts along dimension 1
There are 2 independent parts, one for each index of `groups`. A program takes and returns all parts, laid end to end along the dimension named above; each array names one. Nothing has to cross between parts.
All inputs are finite; a program needn't handle non-finite values.
Results may differ from a plain program's by a relative error of at most 0.00017.
Values sent between devices are 32-bit elements; how exact they have to be, the bound alone decides.
No kernel may reach another device: no remote copies, remote signals or barrier semaphores. Data moves between devices by JAX's collectives and lax.ppermute only.
A program may use at most 64 MiB of HBM per device.

v0:
```python
import functools
import math

import jax
import jax.numpy as jnp
import ml_dtypes
import numpy as np
from jax import lax
from jax.experimental import pallas as pl
from jax.experimental.pallas import tpu as pltpu
from jax.sharding import PartitionSpec as P

SUBSTEPS = 4
ZOOM = 4
LEVELS = 16
PLATE = 32

DIFFRACT = (0.08, 0.04, 0.027)
WALKOFF = (0.3, -0.8, 0.8)
COUPLE = (0.08, 0.16, 0.24)
FAR_SCALE = 4.0

UNITS = tuple(
    math.sqrt(COUPLE[j] / (COUPLE[0] * COUPLE[1] * COUPLE[2])) for j in range(3)
)
HALO = 2 * SUBSTEPS
TILE = 8
LANES = 128
F32 = jnp.float32
BF16 = jnp.bfloat16


def split_table(table):
    high = table.astype(np.float32).astype(ml_dtypes.bfloat16)
    low = (table - high.astype(np.float64)).astype(np.float32).astype(ml_dtypes.bfloat16)
    return high, low


def row_tables(rows, far_rows, scale):
    u = np.arange(far_rows, dtype=np.int64) - far_rows // 2
    y = np.arange(rows, dtype=np.int64) - rows // 2
    period = ZOOM * rows
    angle = 2.0 * np.pi / period * np.mod(u[:, None] * y[None, :], period)
    real, imaginary = scale * np.cos(angle), -scale * np.sin(angle)
    forward = np.concatenate([real, imaginary], axis=1)
    backward = np.concatenate([real.T, imaginary.T], axis=1)
    return split_table(forward), split_table(backward)


def column_tables(far_columns):
    v = np.arange(far_columns, dtype=np.int64)
    angle = 2.0 * np.pi / far_columns * np.mod(v[:, None] * v[None, :], far_columns)
    return split_table(np.concatenate([np.cos(angle), np.sin(angle)], axis=1))


def split(value):
    high = value.astype(BF16)
    low = (value - high.astype(F32)).astype(BF16)
    return high, low


def dot(left, right):
    return jnp.dot(left, right, preferred_element_type=F32)


def plate_phase(levels):
    count, across = levels.shape
    block = lax.broadcasted_iota(jnp.int32, (count, across * PLATE), 1) // PLATE
    level = jnp.zeros((count, across * PLATE), F32)
    for b in range(across):
        level = jnp.where(block == b, levels[:, b : b + 1].astype(F32), level)
    angle = (2.0 * math.pi / LEVELS) * level
    return jnp.cos(angle), jnp.sin(angle)


def edges_kernel(one_ref, two_ref, mismatch_ref, turned_ref, near_ref, far_ref):
    halves = one_ref.shape[1] // LANES
    width = one_ref.shape[2]
    even = lax.rem(lax.axis_index("gx"), 2) == 0
    for c in range(5):
        for h in range(halves):
            rows = pl.ds(h * LANES, LANES)
            if c < 2:
                block = one_ref[c, rows, :] * (1.0 / UNITS[0])
            elif c < 4:
                block = two_ref[c - 2, rows, :] * (1.0 / UNITS[1])
            else:
                block = mismatch_ref[rows, :]
            block = block.T
            turned_ref[c, h] = block
            first, last = block[:HALO], block[width - HALO :]
            near_ref[c, h] = jnp.where(even, last, first)
            far_ref[c, h] = jnp.where(even, first, last)


def sine_pair(angle):
    q = angle * angle
    sine = jnp.full_like(q, 1.0 / math.factorial(15) * -1.0)
    cosine = jnp.full_like(q, 1.0 / math.factorial(16))
    for k in (13, 11, 9, 7, 5, 3, 1):
        sine = sine * q + (-1.0) ** (k // 2) / math.factorial(k)
    for k in (14, 12, 10, 8, 6, 4, 2, 0):
        cosine = cosine * q + (-1.0) ** (k // 2) / math.factorial(k)
    return cosine, sine * angle


def cmul(a, b):
    return a[0] * b[0] - a[1] * b[1], a[0] * b[1] + a[1] * b[0]


def cmul_conj(a, b):
    return a[0] * b[0] + a[1] * b[1], a[1] * b[0] - a[0] * b[1]


def advance(source, row, halves, turn, start, waves):
    lane = lax.broadcasted_iota(jnp.int32, (TILE, LANES), 1)
    used = range(4) if start else range(6)
    mid = [[source[c, h, pl.ds(row, TILE), :] for h in range(halves)] for c in used]
    linear = {}
    for wave in waves:
        if start and wave == 2:
            continue
        side = -1 if WALKOFF[wave] > 0 else 1
        drift, spread = abs(WALKOFF[wave]), DIFFRACT[wave]
        for part in range(2):
            c = 2 * wave + part
            up = [pltpu.roll(m, 1, 1) for m in mid[c]]
            down = [pltpu.roll(m, LANES - 1, 1) for m in mid[c]]
            for h in range(halves):
                above = jnp.where(lane == 0, up[h - 1] if h else 0.0, up[h])
                beyond = down[h + 1] if h + 1 < halves else 0.0
                below = jnp.where(lane == LANES - 1, beyond, down[h])
                left = source[c, h, pl.ds(row - 1, TILE), :]
                right = source[c, h, pl.ds(row + 1, TILE), :]
                around = (above + below) + (left + right)
                m = mid[c][h]
                bend = spread * around - (4.0 * spread) * m
                move = (1.0 - drift) * m + drift * (left if side < 0 else right)
                linear[c, h] = (bend, move)
    out = {}
    for h in range(halves):
        a1, a2 = (mid[0][h], mid[1][h]), (mid[2][h], mid[3][h])
        mixes = {}
        if start:
            mixes[2] = cmul(a1, a2)
        else:
            a3 = (mid[4][h], mid[5][h])
            phase = turn(h)
            if 0 in waves:
                back = cmul_conj(a3, phase) if phase is not None else a3
                mixes[0] = cmul_conj(back, a2)
                mixes[1] = cmul_conj(back, a1)
            ahead = cmul(a1, phase) if phase is not None else a1
            mixes[2] = cmul(ahead, a2)
        for wave in waves:
            real, imaginary = 2 * wave, 2 * wave + 1
            mix = mixes.get(wave)
            if (real, h) not in linear:
                out[real, h], out[imaginary, h] = -mix[1], mix[0]
                continue
            real_part = linear[real, h][1] - linear[imaginary, h][0]
            imaginary_part = linear[imaginary, h][1] + linear[real, h][0]
            if mix is not None:
                real_part = real_part - mix[1]
                imaginary_part = imaginary_part + mix[0]
            out[real, h], out[imaginary, h] = real_part, imaginary_part
    return out


def crystal_kernel(
    turned_ref, near_ref, far_ref, plate_ref, high_ref, low_ref,
    third_ref, sent_ref,
    field, trial, angles, result,
):
    halves, width = turned_ref.shape[1], turned_ref.shape[2]
    devices = sent_ref.shape[0]
    index = lax.axis_index("gx")
    even = lax.rem(index, 2) == 0
    tiles = width // TILE + 2
    begin = 2 * TILE
    keep_first = jnp.where(index > 0, 1.0, 0.0).astype(F32)
    keep_last = jnp.where(index < devices - 1, 1.0, 0.0).astype(F32)

    zero = jnp.zeros((TILE, LANES), F32)
    for h in range(halves):
        for c in range(6):
            for at in (0, (tiles + 1) * TILE):
                field[c, h, pl.ds(at, TILE), :] = zero
                trial[c, h, pl.ds(at, TILE), :] = zero
        for c in range(4):
            field[c, h, pl.ds(begin, width), :] = turned_ref[c, h]
            a, b = near_ref[c, h], far_ref[c, h]
            field[c, h, pl.ds(TILE, TILE), :] = jnp.where(even, b, a) * keep_first
            field[c, h, pl.ds(begin + width, TILE), :] = jnp.where(even, a, b) * keep_last

    def store_angles(h, row, value):
        c1, s1 = sine_pair(value)
        one = (c1, s1)
        two = (c1 * c1 - s1 * s1, 2.0 * c1 * s1)
        three = cmul(one, two)
        four = (two[0] * two[0] - two[1] * two[1], 2.0 * two[0] * two[1])
        for z, pair in enumerate((one, two, three, four)):
            angles[2 * z, h, pl.ds(row, TILE), :] = pair[0]
            angles[2 * z + 1, h, pl.ds(row, TILE), :] = pair[1]

    for h in range(halves):
        a, b = near_ref[4, h], far_ref[4, h]
        store_angles(h, TILE, jnp.where(even, b, a))
        store_angles(h, begin + width, jnp.where(even, a, b))

    def angle_body(t, carry):
        for h in range(halves):
            row = pl.multiple_of(t * TILE, TILE)
            store_angles(h, pl.multiple_of(row + begin, TILE), turned_ref[4, h, pl.ds(row, TILE), :])
        return carry

    lax.fori_loop(0, width // TILE, angle_body, 0, unroll=2)

    def turn_at(z, row):
        def turn(h):
            if z == 0:
                return None
            return tuple(angles[2 * (z - 1) + k, h, pl.ds(row, TILE), :] for k in range(2))

        return turn

    def first_half(step, row, keep):
        out = advance(field, row, halves, turn_at(step, row), step == 0, range(3))
        for (c, h), value in out.items():
            trial[c, h, pl.ds(row, TILE), :] = value if keep is None else value * keep

    def second_half(step, row, keep):
        last = step == SUBSTEPS - 1
        waves = (2,) if last else range(3)
        out = advance(trial, row, halves, turn_at(step + 1, row), False, waves)
        for (c, h), value in out.items():
            if step == 0 and c >= 4:
                value = 0.5 * value
            else:
                value = 0.5 * (field[c, h, pl.ds(row, TILE), :] + value)
            if last:
                at = pl.multiple_of(row - begin, TILE)
                result[c - 4, h, pl.ds(at, TILE), :] = value * UNITS[2]
            else:
                field[c, h, pl.ds(row, TILE), :] = value if keep is None else value * keep

    def sweep(half, step, edges):
        if edges:
            half(step, TILE, keep_first)
            half(step, tiles * TILE, keep_last)

        def body(t, carry):
            half(step, pl.multiple_of(begin + t * TILE, TILE), None)
            return carry

        lax.fori_loop(0, width // TILE, body, 0, unroll=2)

    for step in range(SUBSTEPS):
        sweep(first_half, step, True)
        sweep(second_half, step, step < SUBSTEPS - 1)

    cosine, sine_part = plate_phase(plate_ref[...])
    parts = [[], []]
    for h in range(halves):
        blocks = [result[p, h].T for p in range(2)]
        for p in range(2):
            third_ref[p, pl.ds(h * LANES, LANES), :] = blocks[p]
        for k in range(LANES // PLATE):
            at = h * (LANES // PLATE) + k
            turn = (cosine[at : at + 1], sine_part[at : at + 1])
            piece = [b[k * PLATE : (k + 1) * PLATE] for b in blocks]
            product = cmul(piece, turn)
            for p in range(2):
                parts[p].append(product[p])
    real, imaginary = (jnp.concatenate(p, axis=0) for p in parts)
    data = jnp.concatenate(
        [jnp.concatenate([real, imaginary], axis=1), jnp.concatenate([-imaginary, real], axis=1)],
        axis=0,
    )
    high, low = split(data)
    spectrum = dot(high_ref[...], high) + (dot(high_ref[...], low) + dot(low_ref[...], high))
    share = spectrum.shape[0] // devices
    for d in range(devices):
        for p in range(2):
            sent_ref[d, p] = spectrum[d * share : (d + 1) * share, p * width : (p + 1) * width]


def spot_kernel(
    got_ref, low_ref, high_ref, row_ref, column_ref, table_high_ref, table_low_ref,
    far_ref, sent_ref,
):
    devices, _, share, width = got_ref.shape
    columns = column_ref.shape[1]
    classes = columns // width
    first = lax.axis_index("gx") * share

    folded = []
    for p in range(2):
        pieces = []
        for k in range(classes):
            terms = [got_ref[d, p] for d in range(k, devices, classes)]
            while len(terms) > 1:
                terms = [sum(terms[i : i + 2]) for i in range(0, len(terms), 2)]
            pieces.append(terms[0])
        folded.append(jnp.concatenate(pieces, axis=1))
    position = lax.broadcasted_iota(jnp.int32, (2 * share, columns), 1)
    parity = (1 - 2 * lax.rem(position, 2)).astype(F32)

    def transform(stacked):
        high, low = split(stacked)
        both = dot(jnp.concatenate([high, low], axis=0), table_high_ref[...])
        total = both[: 2 * share] + (both[2 * share :] + dot(high, table_low_ref[...]))
        return total[:, :columns], total[:, columns:]

    cosines, sines = transform(jnp.concatenate(folded, axis=0) * parity)
    far_real = cosines[:share] + sines[share:]
    far_imaginary = cosines[share:] - sines[:share]
    far_ref[0] = far_real
    far_ref[1] = far_imaginary

    rows = low_ref.shape[1]
    own = lax.broadcasted_iota(jnp.int32, (share, rows), 1) == first + lax.broadcasted_iota(
        jnp.int32, (share, rows), 0
    )

    def own_rows(ref):
        value = jnp.where(own, ref[...].astype(F32), 0.0)
        return jnp.sum(value, axis=1, keepdims=True)

    spot = lax.broadcasted_iota(jnp.int32, (share, columns), 1).astype(F32)
    inside = (spot >= own_rows(low_ref)) & (spot < own_rows(high_ref))
    gain = own_rows(row_ref) * column_ref[...]
    power = far_real * far_real + far_imaginary * far_imaginary
    factor = jnp.where(inside, gain * lax.rsqrt(jnp.maximum(power, 1.0)), 1.0)
    replaced = jnp.concatenate([far_real * factor, far_imaginary * factor], axis=0)
    cosines, sines = transform(replaced)
    parity = parity[:share]
    across = (
        (cosines[:share] - sines[share:]) * parity,
        (cosines[share:] + sines[:share]) * parity,
    )
    for d in range(devices):
        k = d % classes
        for p in range(2):
            sent_ref[d, p] = across[p][:, k * width : (k + 1) * width]


def back_kernel(got_ref, plate_ref, high_ref, low_ref, back_ref):
    devices, _, share, width = got_ref.shape
    real = got_ref[:, 0].reshape(devices * share, width)
    imaginary = got_ref[:, 1].reshape(devices * share, width)
    data = jnp.concatenate(
        [jnp.concatenate([real, imaginary], axis=1), jnp.concatenate([imaginary, -real], axis=1)],
        axis=0,
    )
    high, low = split(data)
    total = dot(high_ref[...], high) + (dot(high_ref[...], low) + dot(low_ref[...], high))
    cosine, sine_part = plate_phase(plate_ref[...])
    for k in range(total.shape[0] // PLATE):
        rows = slice(k * PLATE, (k + 1) * PLATE)
        piece = (total[rows, :width], total[rows, width:])
        turn = (cosine[k : k + 1], sine_part[k : k + 1])
        product = cmul_conj(piece, turn)
        for p in range(2):
            back_ref[p, rows, :] = product[p]


def shape(*dims):
    return jax.ShapeDtypeStruct(dims, F32)


def local(wave_one, wave_two, mismatch, plate, spot_low, spot_high, row_gain, column_gain):
    devices = lax.axis_size("gx")
    rows, width = wave_one.shape[1:]
    far_rows, far_columns = row_gain.shape[0], column_gain.shape[0]
    whole_width = width * devices
    halves = rows // LANES
    share = far_rows // devices
    assert rows % LANES == 0 and width == LANES
    assert far_columns % width == 0 and devices % (far_columns // width) == 0
    assert (whole_width // 2) % far_columns == 0 and devices % 2 == 0
    scale = FAR_SCALE / math.sqrt(rows * whole_width)
    forward, backward = row_tables(rows, far_rows, scale)
    columns = column_tables(far_columns)

    strip = shape(5, halves, HALO, LANES)
    turned, near, far = pl.pallas_call(
        edges_kernel, out_shape=(shape(5, halves, width, LANES), strip, strip), name="edges"
    )(wave_one, wave_two, mismatch)
    near = lax.ppermute(near, "gx", [(i, i ^ 1) for i in range(devices)])
    pairs = [(i, i + 1) for i in range(1, devices - 1, 2)]
    far = lax.ppermute(far, "gx", pairs + [(j, i) for i, j in pairs])

    length = width + 4 * TILE
    third, sent = pl.pallas_call(
        crystal_kernel,
        out_shape=(shape(2, rows, width), shape(devices, 2, share, width)),
        scratch_shapes=[
            pltpu.VMEM((6, halves, length, LANES), F32),
            pltpu.VMEM((6, halves, length, LANES), F32),
            pltpu.VMEM((2 * SUBSTEPS, halves, length, LANES), F32),
            pltpu.VMEM((2, halves, width, LANES), F32),
        ],
        name="crystal",
    )(turned, near, far, plate, *forward)
    got = lax.all_to_all(sent, "gx", 0, 0, tiled=True)
    far_field, sent = pl.pallas_call(
        spot_kernel,
        out_shape=(shape(2, share, far_columns), shape(devices, 2, share, width)),
        name="spot",
    )(
        got,
        spot_low.reshape(1, far_rows),
        spot_high.reshape(1, far_rows),
        row_gain.reshape(1, far_rows),
        column_gain.reshape(1, far_columns),
        *columns,
    )
    got = lax.all_to_all(sent, "gx", 0, 0, tiled=True)
    back = pl.pallas_call(back_kernel, out_shape=shape(2, rows, width), name="back")(
        got, plate, *backward
    )
    return third, far_field, back


def solution(mesh):
    return jax.shard_map(
        local,
        mesh=mesh,
        in_specs=(
            P(None, "groups", "gx"),
            P(None, "groups", "gx"),
            P("groups", "gx"),
            P("groups", "gx"),
            P("groups"),
            P("groups"),
            P("groups"),
            P("groups"),
        ),
        out_specs=(
            P(None, "groups", "gx"),
            P(None, ("groups", "gx"), None),
            P(None, "groups", "gx"),
        ),
        check_vma=False,
    )
```

profile of v0, /device:TPU:0, one launch (start us, length us, event | category | flops | bytes accessed | tf_op | source)
XLA Modules:
  0.0 67.4 jit_solution(17662913390393067175)
XLA Ops:
  0.6 2.1 %edges.1 = (f32[5,2,128,128]{3,2,1,0:T(8,128)}, f32[5,2,8,128]{3,2,1,0:T(8,128)}, f32[5,2,8,128]{3,2,1,0:T(8,128)}) custom-call(f32[2,256,128]{2,1,0:T(8,128)} %one_ref.1, f32[2,256,128]{2,1,0:T(8,128)} %two_ref.1, f32[256,128]{1,0:T(8,128)} %mismatch_ref.1), custom_call_target="tpu_custom_call" | custom-call | tf_op jit(solution)/shard_map/edges/pallas_call | solution.py:387
  2.8 0.0 copy-start.2
  2.8 0.5 collective-permute-start
  3.3 0.7 collective-permute-start.1
  3.9 0.0 copy-done.2
  3.9 0.7 copy.17.plate_ref
  4.6 0.0 collective-permute-done.near_ref
  4.6 0.0 copy-start
  4.6 0.0 collective-permute-done.1.far_ref
  4.6 0.0 copy-start.1
  4.6 0.6 copy-done
  5.2 0.0 copy-done.1
  5.2 11.9 %crystal.1 = (f32[2,256,128]{2,1,0:T(8,128)}, f32[16,2,32,128]{3,2,1,0:T(8,128)}) custom-call(f32[5,2,128,128]{3,2,1,0:T(8,128)} %get-tuple-element.10.turned_ref, f32[5,2,8,128]{3,2,1,0:T(8,128)} %copy-done, f32[5,2,8,128]{3,2,1,0:T(8,128)} %copy-done.1, s32[8,4]{1,0:T(8,128)} %copy.17.plate_ref, bf16[512,512]{1,0:T(8,128)(2,1)} %constant.12.clone.high_ref, ...), custom_call_target="tpu_custom_call" | custom-call | tf_op jit(solution)/shard_map/crystal/pallas_call | solution.py:395
  17.1 25.6 %all_to_all.10.got_ref = f32[16,2,32,128]{3,2,1,0:T(8,128)} all-to-all(f32[16,2,32,128]{3,2,1,0:T(8,128)} %get-tuple-element.14), channel_id=1, replica_groups=mesh['groups'=2,'gx'=16] {'gx'}, dimensions={0} | all-to-all | bytes 1048576 | tf_op jit(solution)/shard_map/all_to_all | solution.py:406
  42.7 3.5 %spot.1 = (f32[2,32,512]{2,1,0:T(8,128)}, f32[16,2,32,128]{3,2,1,0:T(8,128)}) custom-call(f32[16,2,32,128]{3,2,1,0:T(8,128)} %all_to_all.10.got_ref, s32[1,512]{1,0:T(1,128)} %bitcast.4, s32[1,512]{1,0:T(1,128)} %bitcast.5, f32[1,512]{1,0:T(1,128)} %bitcast.6, f32[1,512]{1,0:T(1,128)} %bitcast.7, bf16[512,1024]{1,0:T(8,128)(2,1)} %constant.14.clone.table_high_ref, ...), custom_call_target="tpu_custom_call" | custom-call | tf_op jit(solution)/shard_map/spot/pallas_call | solution.py:407
  46.2 18.5 %all_to_all.11.got_ref = f32[16,2,32,128]{3,2,1,0:T(8,128)} all-to-all(f32[16,2,32,128]{3,2,1,0:T(8,128)} %get-tuple-element.16), channel_id=1, replica_groups=mesh['groups'=2,'gx'=16] {'gx'}, dimensions={0} | all-to-all | bytes 1048576 | tf_op jit(solution)/shard_map/all_to_all | solution.py:419
  64.8 2.6 %back.1 = f32[2,256,128]{2,1,0:T(8,128)} custom-call(f32[16,2,32,128]{3,2,1,0:T(8,128)} %all_to_all.11.got_ref, s32[8,4]{1,0:T(8,128)} %copy.17.plate_ref, bf16[256,1024]{1,0:T(8,128)(2,1)} %constant.16.clone.high_ref, bf16[256,1024]{1,0:T(8,128)(2,1)} %constant.17.clone.low_ref), custom_call_target="tpu_custom_call" | custom-call | tf_op jit(solution)/shard_map/back/pallas_call | solution.py:420
Async XLA Ops:
  2.8 1.2 %copy-start.2 = (s32[8,4]{0,1:T(4,128)S(1)}, s32[8,4]{0,1:T(4,128)}, u32[]{:S(2)}) copy-start(s32[8,4]{0,1:T(4,128)} %param.17) | copy-start | bytes 388
  2.8 1.8 %collective-permute-start = (f32[5,2,8,128]{3,2,1,0:T(8,128)}, f32[5,2,8,128]{3,2,1,0:T(8,128)S(1)}, u32[]{:S(2)}, u32[]{:S(2)}) collective-permute-start(f32[5,2,8,128]{3,2,1,0:T(8,128)} %get-tuple-element.11), channel_id=1, source_target_pairs={{0,1},{1,0},{2,3},{3,2},{4,5},{5,4},{6,7},{7,6},{8,9},{9,8},{10,11... | collective-permute-start | bytes 122888 | tf_op jit(solution)/shard_map/ppermute | solution.py:390
  3.3 1.4 %collective-permute-start.1 = (f32[5,2,8,128]{3,2,1,0:T(8,128)}, f32[5,2,8,128]{3,2,1,0:T(8,128)S(1)}, u32[]{:S(2)}, u32[]{:S(2)}) collective-permute-start(f32[5,2,8,128]{3,2,1,0:T(8,128)} %get-tuple-element.12), channel_id=1, source_target_pairs={{1,2},{3,4},{5,6},{7,8},{9,10},{11,12},{13,14},{2,1},{4,3},{6,5},{... | collective-permute-start | bytes 122888 | tf_op jit(solution)/shard_map/ppermute | solution.py:392
  4.6 0.6 copy-start
  4.6 0.6 copy-start.1
where the time goes:
time: 67.9 us; the launch traced here: 67.4 us
  blocking collectives  44.2 us (65%)
  Pallas kernels  20.1 us (30%)
  local copies, waits for them, and re-layouts  1.29 us (2%)
  starting transfers between devices  1.14 us (2%)
    all_to_all x2, blocking collectives, local(): got = lax.all_to_all(sent, 'gx', 0, 0, tiled=True)  44.2 us
    pallas_call x1, Pallas kernels, local(): pl.pallas_call(crystal_kernel, out_shape=(shape(2, rows, width), shape(de...  11.9 us
    pallas_call x1, Pallas kernels, local(): pl.pallas_call(spot_kernel, out_shape=(shape(2, share, far_columns), shap...  3.49 us
    pallas_call x1, Pallas kernels, local(): pl.pallas_call(back_kernel, out_shape=shape(2, rows, width), name='back')  2.65 us
    pallas_call x1, Pallas kernels, local(): pl.pallas_call(edges_kernel, out_shape=(shape(5, halves, width, LANES), s...  2.15 us
  transfers between devices with their start and end apart: 2, of which 0 were waited for; matrix products, arithmetic and copies ran while one was open for 1% of the time, Pallas kernels for 0%

commit v1 on v0

--- a/solution.py
+++ b/solution.py
@@ -25,6 +25,7 @@
 )
 HALO = 2 * SUBSTEPS
 TILE = 8
+GROUPS = 1
 LANES = 128
 F32 = jnp.float32
 BF16 = jnp.bfloat16
@@ -42,7 +43,9 @@
     period = ZOOM * rows
     angle = 2.0 * np.pi / period * np.mod(u[:, None] * y[None, :], period)
     real, imaginary = scale * np.cos(angle), -scale * np.sin(angle)
-    forward = np.concatenate([real, imaginary], axis=1)
+    halves = rows // LANES
+    order = np.arange(rows).reshape(LANES, halves).T.reshape(-1)
+    forward = np.concatenate([real[:, order], imaginary[:, order]], axis=1)
     backward = np.concatenate([real.T, imaginary.T], axis=1)
     return split_table(forward), split_table(backward)
 
@@ -73,13 +76,30 @@
     return jnp.cos(angle), jnp.sin(angle)
 
 
-def edges_kernel(one_ref, two_ref, mismatch_ref, turned_ref, near_ref, far_ref):
+def start_copies(sources, targets, sems):
+    copies = [
+        pltpu.make_async_copy(a, b, sems.at[i]) for i, (a, b) in enumerate(zip(sources, targets))
+    ]
+    for copy in copies:
+        copy.start()
+    return copies
+
+
+def edges_kernel(
+    one_hbm, two_hbm, mismatch_hbm, turned_ref, near_ref, far_ref,
+    one_ref, two_ref, mismatch_ref, sems,
+):
     halves = one_ref.shape[1] // LANES
     width = one_ref.shape[2]
+    copies = start_copies(
+        (one_hbm, two_hbm, mismatch_hbm), (one_ref, two_ref, mismatch_ref), sems
+    )
     even = lax.rem(lax.axis_index("gx"), 2) == 0
     for c in range(5):
+        if c % 2 == 0:
+            copies[c // 2].wait()
         for h in range(halves):
-            rows = pl.ds(h * LANES, LANES)
+            rows = pl.ds(h, LANES, stride=halves)
             if c < 2:
                 block = one_ref[c, rows, :] * (1.0 / UNITS[0])
             elif c < 4:
@@ -95,11 +115,11 @@
 
 def sine_pair(angle):
     q = angle * angle
-    sine = jnp.full_like(q, 1.0 / math.factorial(15) * -1.0)
-    cosine = jnp.full_like(q, 1.0 / math.factorial(16))
-    for k in (13, 11, 9, 7, 5, 3, 1):
+    sine = (1.0 / math.factorial(13)) * q - 1.0 / math.factorial(11)
+    cosine = (-1.0 / math.factorial(14)) * q + 1.0 / math.factorial(12)
+    for k in (9, 7, 5, 3, 1):
         sine = sine * q + (-1.0) ** (k // 2) / math.factorial(k)
-    for k in (14, 12, 10, 8, 6, 4, 2, 0):
+    for k in (10, 8, 6, 4, 2, 0):
         cosine = cosine * q + (-1.0) ** (k // 2) / math.factorial(k)
     return cosine, sine * angle
 
@@ -124,12 +144,11 @@
         drift, spread = abs(WALKOFF[wave]), DIFFRACT[wave]
         for part in range(2):
             c = 2 * wave + part
-            up = [pltpu.roll(m, 1, 1) for m in mid[c]]
-            down = [pltpu.roll(m, LANES - 1, 1) for m in mid[c]]
+            wrap = jnp.where(lane == 0, 0.0, pltpu.roll(mid[c][-1], 1, 1))
+            over = jnp.where(lane == LANES - 1, 0.0, pltpu.roll(mid[c][0], LANES - 1, 1))
             for h in range(halves):
-                above = jnp.where(lane == 0, up[h - 1] if h else 0.0, up[h])
-                beyond = down[h + 1] if h + 1 < halves else 0.0
-                below = jnp.where(lane == LANES - 1, beyond, down[h])
+                above = mid[c][h - 1] if h else wrap
+                below = mid[c][h + 1] if h + 1 < halves else over
                 left = source[c, h, pl.ds(row - 1, TILE), :]
                 right = source[c, h, pl.ds(row + 1, TILE), :]
                 around = (above + below) + (left + right)
@@ -168,10 +187,11 @@
 
 
 def crystal_kernel(
-    turned_ref, near_ref, far_ref, plate_ref, high_ref, low_ref,
-    third_ref, sent_ref,
-    field, trial, angles, result,
+    turned_ref, near_ref, far_ref, plate_ref, high_hbm, low_hbm, *rest
 ):
+    spots, (third_ref, sent_ref), rest = rest[:4], rest[4:6], rest[6:]
+    kept, (field, trial, angles, result, high_ref, low_ref, sems) = rest[:4], rest[4:]
+    copies = start_copies((high_hbm, low_hbm, *spots), (high_ref, low_ref, *kept), sems)
     halves, width = turned_ref.shape[1], turned_ref.shape[2]
     devices = sent_ref.shape[0]
     index = lax.axis_index("gx")
@@ -200,8 +220,10 @@
         three = cmul(one, two)
         four = (two[0] * two[0] - two[1] * two[1], 2.0 * two[0] * two[1])
         for z, pair in enumerate((one, two, three, four)):
-            angles[2 * z, h, pl.ds(row, TILE), :] = pair[0]
-            angles[2 * z + 1, h, pl.ds(row, TILE), :] = pair[1]
+            for late in range(2 if z < 3 else 1):
+                at, unit = 4 * z + 2 * late, 0.5 ** (z + late)
+                for k in range(2):
+                    angles[at + k, h, pl.ds(row, TILE), :] = unit * pair[k]
 
     for h in range(halves):
         a, b = near_ref[4, h], far_ref[4, h]
@@ -216,44 +238,48 @@
 
     lax.fori_loop(0, width // TILE, angle_body, 0, unroll=2)
 
-    def turn_at(z, row):
+    def turn_at(z, late, row):
         def turn(h):
             if z == 0:
                 return None
-            return tuple(angles[2 * (z - 1) + k, h, pl.ds(row, TILE), :] for k in range(2))
+            at = 4 * (z - 1) + 2 * late
+            return tuple(angles[at + k, h, pl.ds(row, TILE), :] for k in range(2))
 
         return turn
 
     def first_half(step, row, keep):
-        out = advance(field, row, halves, turn_at(step, row), step == 0, range(3))
+        out = advance(field, row, halves, turn_at(step, 1, row), step == 0, range(3))
         for (c, h), value in out.items():
             trial[c, h, pl.ds(row, TILE), :] = value if keep is None else value * keep
 
     def second_half(step, row, keep):
         last = step == SUBSTEPS - 1
         waves = (2,) if last else range(3)
-        out = advance(trial, row, halves, turn_at(step + 1, row), False, waves)
+        out = advance(trial, row, halves, turn_at(step + 1, 0, row), False, waves)
         for (c, h), value in out.items():
-            if step == 0 and c >= 4:
-                value = 0.5 * value
-            else:
-                value = 0.5 * (field[c, h, pl.ds(row, TILE), :] + value)
+            if step > 0 or c < 4:
+                value = field[c, h, pl.ds(row, TILE), :] + value
             if last:
                 at = pl.multiple_of(row - begin, TILE)
-                result[c - 4, h, pl.ds(at, TILE), :] = value * UNITS[2]
+                result[c - 4, h, pl.ds(at, TILE), :] = value * (UNITS[2] * 0.5**SUBSTEPS)
             else:
                 field[c, h, pl.ds(row, TILE), :] = value if keep is None else value * keep
 
     def sweep(half, step, edges):
-        if edges:
-            half(step, TILE, keep_first)
-            half(step, tiles * TILE, keep_last)
+        count, offset = (tiles, TILE) if edges else (tiles - 2, begin)
+        group = count // GROUPS
 
         def body(t, carry):
-            half(step, pl.multiple_of(begin + t * TILE, TILE), None)
+            for j in range(group):
+                keep = None
+                if edges and j == 0:
+                    keep = jnp.where(t == 0, keep_first, 1.0)
+                elif edges and j == group - 1:
+                    keep = jnp.where(t == GROUPS - 1, keep_last, 1.0)
+                half(step, pl.multiple_of(offset + (t * group + j) * TILE, TILE), keep)
             return carry
 
-        lax.fori_loop(0, width // TILE, body, 0, unroll=2)
+        lax.fori_loop(0, GROUPS, body, 0)
 
     for step in range(SUBSTEPS):
         sweep(first_half, step, True)
@@ -264,11 +290,11 @@
     for h in range(halves):
         blocks = [result[p, h].T for p in range(2)]
         for p in range(2):
-            third_ref[p, pl.ds(h * LANES, LANES), :] = blocks[p]
-        for k in range(LANES // PLATE):
-            at = h * (LANES // PLATE) + k
-            turn = (cosine[at : at + 1], sine_part[at : at + 1])
-            piece = [b[k * PLATE : (k + 1) * PLATE] for b in blocks]
+            third_ref[p, pl.ds(h, LANES, stride=halves), :] = blocks[p]
+        run = PLATE // halves
+        for k in range(LANES // run):
+            turn = (cosine[k : k + 1], sine_part[k : k + 1])
+            piece = [b[k * run : (k + 1) * run] for b in blocks]
             product = cmul(piece, turn)
             for p in range(2):
                 parts[p].append(product[p])
@@ -278,6 +304,8 @@
         axis=0,
     )
     high, low = split(data)
+    for copy in copies:
+        copy.wait()
     spectrum = dot(high_ref[...], high) + (dot(high_ref[...], low) + dot(low_ref[...], high))
     share = spectrum.shape[0] // devices
     for d in range(devices):
@@ -286,9 +314,11 @@
 
 
 def spot_kernel(
-    got_ref, low_ref, high_ref, row_ref, column_ref, table_high_ref, table_low_ref,
-    far_ref, sent_ref,
+    got_ref, third_ref, table_high_ref, table_low_ref, low_ref, high_ref, row_ref, column_ref,
+    far_ref, sent_ref, third_hbm,
+    sems,
 ):
+    copies = start_copies((third_ref,), (third_hbm,), sems)
     devices, _, share, width = got_ref.shape
     columns = column_ref.shape[1]
     classes = columns // width
@@ -343,9 +373,12 @@
         k = d % classes
         for p in range(2):
             sent_ref[d, p] = across[p][:, k * width : (k + 1) * width]
-
-
-def back_kernel(got_ref, plate_ref, high_ref, low_ref, back_ref):
+    for copy in copies:
+        copy.wait()
+
+
+def back_kernel(got_ref, far_ref, plate_ref, high_ref, low_ref, back_hbm, far_hbm, back_ref, sems):
+    copies = start_copies((far_ref,), (far_hbm,), sems)
     devices, _, share, width = got_ref.shape
     real = got_ref[:, 0].reshape(devices * share, width)
     imaginary = got_ref[:, 1].reshape(devices * share, width)
@@ -363,10 +396,37 @@
         product = cmul_conj(piece, turn)
         for p in range(2):
             back_ref[p, rows, :] = product[p]
+        if k % 2:
+            done = pl.ds((k - 1) * PLATE, 2 * PLATE)
+            copies += start_copies(
+                (back_ref.at[:, done],), (back_hbm.at[:, done],), sems.at[pl.ds(1 + k // 2, 1)]
+            )
+    for copy in copies:
+        copy.wait()
 
 
 def shape(*dims):
     return jax.ShapeDtypeStruct(dims, F32)
+
+
+def away(array):
+    return pltpu.with_memory_space_constraint(jnp.asarray(array), pltpu.HBM)
+
+
+HELD = pl.BlockSpec(memory_space=pltpu.VMEM)
+AWAY = pl.BlockSpec(memory_space=pltpu.HBM)
+
+
+def call(kernel, name, inputs, outputs, scratch):
+    return pl.pallas_call(
+        kernel,
+        in_specs=inputs,
+        out_specs=[spec for spec, _ in outputs],
+        out_shape=[out for _, out in outputs],
+        scratch_shapes=scratch,
+        compiler_params=pltpu.CompilerParams(vmem_limit_bytes=20 * 2**20),
+        name=name,
+    )
 
 
 def local(wave_one, wave_two, mismatch, plate, spot_low, spot_high, row_gain, column_gain):
@@ -376,50 +436,66 @@
     whole_width = width * devices
     halves = rows // LANES
     share = far_rows // devices
-    assert rows % LANES == 0 and width == LANES
+    assert rows % LANES == 0 and width == LANES and PLATE % halves == 0
+    assert (width // TILE) % GROUPS == 0
     assert far_columns % width == 0 and devices % (far_columns // width) == 0
     assert (whole_width // 2) % far_columns == 0 and devices % 2 == 0
     scale = FAR_SCALE / math.sqrt(rows * whole_width)
     forward, backward = row_tables(rows, far_rows, scale)
     columns = column_tables(far_columns)
 
-    strip = shape(5, halves, HALO, LANES)
-    turned, near, far = pl.pallas_call(
-        edges_kernel, out_shape=(shape(5, halves, width, LANES), strip, strip), name="edges"
-    )(wave_one, wave_two, mismatch)
+    whole = shape(2, rows, width)
+    strip = (HELD, shape(5, halves, HALO, LANES))
+    turned, near, far = call(
+        edges_kernel,
+        "edges",
+        [AWAY] * 3,
+        [(HELD, shape(5, halves, width, LANES)), strip, strip],
+        [
+            pltpu.VMEM((2, rows, width), F32),
+            pltpu.VMEM((2, rows, width), F32),
+            pltpu.VMEM((rows, width), F32),
+            pltpu.SemaphoreType.DMA((3,)),
+        ],
+    )(*(away(a) for a in (wave_one, wave_two, mismatch)))
     near = lax.ppermute(near, "gx", [(i, i ^ 1) for i in range(devices)])
     pairs = [(i, i + 1) for i in range(1, devices - 1, 2)]
     far = lax.ppermute(far, "gx", pairs + [(j, i) for i, j in pairs])
 
     length = width + 4 * TILE
-    third, sent = pl.pallas_call(
+    spots = [a.reshape(1, -1) for a in (spot_low, spot_high, row_gain, column_gain)]
+    chunks = (HELD, shape(devices, 2, share, width))
+    third, sent, *spots = call(
         crystal_kernel,
-        out_shape=(shape(2, rows, width), shape(devices, 2, share, width)),
-        scratch_shapes=[
+        "crystal",
+        [HELD] * 4 + [AWAY] * 6,
+        [(HELD, whole), chunks, *((HELD, jax.ShapeDtypeStruct(a.shape, a.dtype)) for a in spots)],
+        [
             pltpu.VMEM((6, halves, length, LANES), F32),
             pltpu.VMEM((6, halves, length, LANES), F32),
-            pltpu.VMEM((2 * SUBSTEPS, halves, length, LANES), F32),
+            pltpu.VMEM((4 * SUBSTEPS - 2, halves, length, LANES), F32),
             pltpu.VMEM((2, halves, width, LANES), F32),
+            pltpu.VMEM(forward[0].shape, BF16),
+            pltpu.VMEM(forward[1].shape, BF16),
+            pltpu.SemaphoreType.DMA((6,)),
         ],
-        name="crystal",
-    )(turned, near, far, plate, *forward)
+    )(turned, near, far, plate, *(away(a) for a in (*forward, *spots)))
     got = lax.all_to_all(sent, "gx", 0, 0, tiled=True)
-    far_field, sent = pl.pallas_call(
+    far_field, sent, third = call(
         spot_kernel,
-        out_shape=(shape(2, share, far_columns), shape(devices, 2, share, width)),
-        name="spot",
-    )(
-        got,
-        spot_low.reshape(1, far_rows),
-        spot_high.reshape(1, far_rows),
-        row_gain.reshape(1, far_rows),
-        column_gain.reshape(1, far_columns),
-        *columns,
-    )
+        "spot",
+        [HELD] * 8,
+        [(HELD, shape(2, share, far_columns)), chunks, (AWAY, whole)],
+        [pltpu.SemaphoreType.DMA((1,))],
+    )(got, third, *columns, *spots)
     got = lax.all_to_all(sent, "gx", 0, 0, tiled=True)
-    back = pl.pallas_call(back_kernel, out_shape=shape(2, rows, width), name="back")(
-        got, plate, *backward
-    )
+    back, far_field = call(
+        back_kernel,
+        "back",
+        [HELD] * 5,
+        [(AWAY, whole), (AWAY, shape(2, share, far_columns))],
+        [pltpu.VMEM((2, rows, width), F32), pltpu.SemaphoreType.DMA((1 + rows // (2 * PLATE),))],
+    )(got, far_field, plate, *backward)
     return third, far_field, back
 
 

time: 67.9 us -> 54.5 us (0.80)
  Pallas kernels: 20.1 us -> 8.29 us
  local copies, waits for them, and re-layouts: 1.29 us -> 0.11 us
    pallas_call x4, Pallas kernels: 20.1 us -> 8.29 us  [the longest x1 4.71 us: local(): call(crystal_kernel, 'crystal', [HELD] * 4 + [AWAY] * 6, [(HELD, whole),...]
    unnamed x7 -> x11, local copies, waits for them, and re-layouts: 1.29 us -> 0.11 us
  transfers between devices with their start and end apart: 2 -> 2, of which waited for: 0 -> 1; matrix products, arithmetic and copies ran while one was open for 1% -> 0% of each run, Pallas kernels for 0% -> 0%
where the time goes in v1:
time: 54.5 us; the launch traced here: 54.3 us
  blocking collectives  43.9 us (81%)
  Pallas kernels  8.29 us (15%)
  starting transfers between devices  1.21 us (2%)
  between operations  0.7 us (1%)
    all_to_all x2, blocking collectives, local(): got = lax.all_to_all(sent, 'gx', 0, 0, tiled=True)  43.9 us
    pallas_call x1, Pallas kernels, local(): call(crystal_kernel, 'crystal', [HELD] * 4 + [AWAY] * 6, [(HELD, whole),...  4.71 us
    pallas_call x1, Pallas kernels, local(): call(edges_kernel, 'edges', [AWAY] * 3, [(HELD, shape(5, halves, width, L...  1.35 us
    pallas_call x1, Pallas kernels, local(): call(back_kernel, 'back', [HELD] * 5, [(AWAY, whole), (AWAY, shape(2, sha...  1.28 us
  transfers between devices with their start and end apart: 2, of which 1 were waited for; matrix products, arithmetic and copies ran while one was open for 0% of the time, Pallas kernels for 0%

profile of v1, /device:TPU:0, one launch (start us, length us, event | category | flops | bytes accessed | tf_op | source)
XLA Modules:
  0.0 54.3 jit_solution(14593966510064785526)
XLA Ops:
  0.6 1.4 %edges.1 = (f32[5,2,128,128]{3,2,1,0:T(8,128)S(1)}, f32[5,2,8,128]{3,2,1,0:T(8,128)S(1)}, f32[5,2,8,128]{3,2,1,0:T(8,128)S(1)}) custom-call(f32[2,256,128]{2,1,0:T(8,128)} %one_hbm.1, f32[2,256,128]{2,1,0:T(8,128)} %two_hbm.1, f32[256,128]{1,0:T(8,128)} %mismatch_hbm.1), custom_call_target="tpu_custom_call" | custom-call | tf_op jit(solution)/shard_map/edges/pallas_call | solution.py:449
  2.0 0.0 copy-start.4
  2.0 0.6 %collective-permute-start = (f32[5,2,8,128]{3,2,1,0:T(8,128)S(1)}, f32[5,2,8,128]{3,2,1,0:T(8,128)S(1)}, u32[]{:S(2)}, u32[]{:S(2)}) collective-permute-start(f32[5,2,8,128]{3,2,1,0:T(8,128)S(1)} %get-tuple-element.18), channel_id=1, source_target_pairs={{0,1},{1,0},{2,3},{3,2},{4,5},{5,4},{6,7},{7,6},{8,9},{9,8},{10,11... | collective-permute-start | bytes 122888 | tf_op jit(solution)/shard_map/ppermute | solution.py:461
  2.6 0.7 %collective-permute-start.1 = (f32[5,2,8,128]{3,2,1,0:T(8,128)S(1)}, f32[5,2,8,128]{3,2,1,0:T(8,128)S(1)}, u32[]{:S(2)}, u32[]{:S(2)}) collective-permute-start(f32[5,2,8,128]{3,2,1,0:T(8,128)S(1)} %get-tuple-element.19), channel_id=1, source_target_pairs={{1,2},{3,4},{5,6},{7,8},{9,10},{11,12},{13,14},{2,1},{4,3},{6,5},{... | collective-permute-start | bytes 122888 | tf_op jit(solution)/shard_map/ppermute | solution.py:463
  3.2 0.0 copy-done.4
  3.2 0.1 copy.17.plate_ref
  3.3 0.1 collective-permute-done.near_ref
  3.4 0.0 collective-permute-done.1.far_ref
  3.4 0.0 copy-start
  3.4 0.0 copy-start.1
  3.4 4.7 %crystal.1 = (f32[2,256,128]{2,1,0:T(8,128)S(1)}, f32[16,2,32,128]{3,2,1,0:T(8,128)S(1)}, s32[1,512]{1,0:T(1,128)S(1)}, s32[1,512]{1,0:T(1,128)S(1)}, f32[1,512]{1,0:T(1,128)S(1)}, /*index=5*/f32[1,512]{1,0:T(1,128)S(1)}) custom-call(f32[5,2,128,128]{3,2,1,0:T(8,128)S(1)} %get-tuple-element.17.turned_ref, ...), custom_call_target="tpu_custom_call" | custom-call | tf_op jit(solution)/shard_map/crystal/pallas_call | solution.py:468
  8.2 25.5 %all_to_all.10.got_ref = f32[16,2,32,128]{3,2,1,0:T(8,128)S(1)} all-to-all(f32[16,2,32,128]{3,2,1,0:T(8,128)S(1)} %get-tuple-element.20), channel_id=1, replica_groups=mesh['groups'=2,'gx'=16] {'gx'}, dimensions={0} | all-to-all | bytes 1048576 | tf_op jit(solution)/shard_map/all_to_all | solution.py:483
  33.7 0.0 copy-done
  33.7 0.0 copy-done.1
  33.7 0.9 %spot.1 = (f32[2,32,512]{2,1,0:T(8,128)S(1)}, f32[16,2,32,128]{3,2,1,0:T(8,128)S(1)}, f32[2,256,128]{2,1,0:T(8,128)}) custom-call(f32[16,2,32,128]{3,2,1,0:T(8,128)S(1)} %all_to_all.10.got_ref, f32[2,256,128]{2,1,0:T(8,128)S(1)} %get-tuple-element.21.third_ref, bf16[512,1024]{1,0:T(8,128)(2,1)S(1)} %copy-done.1, bf16[512,1024]{1,0:T(8,128)(2,1)S(1)} %copy-done, ...), custom_call_target="tpu_custom_call" | custom-call | tf_op jit(solution)/shard_map/spot/pallas_call | solution.py:484
  34.6 0.0 copy-start.2
  34.6 0.0 copy-start.3
  34.6 18.4 %all_to_all.11.got_ref = f32[16,2,32,128]{3,2,1,0:T(8,128)S(1)} all-to-all(f32[16,2,32,128]{3,2,1,0:T(8,128)S(1)} %get-tuple-element.27), channel_id=1, replica_groups=mesh['groups'=2,'gx'=16] {'gx'}, dimensions={0} | all-to-all | bytes 1048576 | tf_op jit(solution)/shard_map/all_to_all | solution.py:491
  53.0 0.0 copy-done.2
  53.0 0.0 copy-done.3
  53.0 1.3 %back.1 = (f32[2,256,128]{2,1,0:T(8,128)}, f32[2,32,512]{2,1,0:T(8,128)}) custom-call(f32[16,2,32,128]{3,2,1,0:T(8,128)S(1)} %all_to_all.11.got_ref, f32[2,32,512]{2,1,0:T(8,128)S(1)} %get-tuple-element.28.far_ref, s32[8,4]{1,0:T(8,128)S(1)} %copy.17.plate_ref, bf16[256,1024]{1,0:T(8,128)(2,1)S(1)} %copy-done.3, bf16[256,1024]{1,0:T(8,128)(2,1)S(1)} %copy-done.2), custom_call_target="tpu_custom_call" | custom-call | tf_op jit(solution)/shard_map/back/pallas_call | solution.py:492
Async XLA Ops:
  2.0 1.2 %copy-start.4 = (s32[8,4]{0,1:T(4,128)S(1)}, s32[8,4]{0,1:T(4,128)}, u32[]{:S(2)}) copy-start(s32[8,4]{0,1:T(4,128)} %param.17) | copy-start | bytes 388
  2.0 1.4 %collective-permute-start = (f32[5,2,8,128]{3,2,1,0:T(8,128)S(1)}, f32[5,2,8,128]{3,2,1,0:T(8,128)S(1)}, u32[]{:S(2)}, u32[]{:S(2)}) collective-permute-start(f32[5,2,8,128]{3,2,1,0:T(8,128)S(1)} %get-tuple-element.18), channel_id=1, source_target_pairs={{0,1},{1,0},{2,3},{3,2},{4,5},{5,4},{6,7},{7,6},{8,9},{9,8},{10,11... | collective-permute-start | bytes 122888 | tf_op jit(solution)/shard_map/ppermute | solution.py:461
  2.6 0.9 %collective-permute-start.1 = (f32[5,2,8,128]{3,2,1,0:T(8,128)S(1)}, f32[5,2,8,128]{3,2,1,0:T(8,128)S(1)}, u32[]{:S(2)}, u32[]{:S(2)}) collective-permute-start(f32[5,2,8,128]{3,2,1,0:T(8,128)S(1)} %get-tuple-element.19), channel_id=1, source_target_pairs={{1,2},{3,4},{5,6},{7,8},{9,10},{11,12},{13,14},{2,1},{4,3},{6,5},{... | collective-permute-start | bytes 122888 | tf_op jit(solution)/shard_map/ppermute | solution.py:463
  3.4 30.2 %copy-start = (bf16[512,1024]{1,0:T(8,128)(2,1)S(1)}, bf16[512,1024]{1,0:T(8,128)(2,1)}, u32[]{:S(2)}) copy-start(bf16[512,1024]{1,0:T(8,128)(2,1)} %constant.15.clone.table_low_ref) | copy-start | bytes 3145732
  3.4 30.2 %copy-start.1 = (bf16[512,1024]{1,0:T(8,128)(2,1)S(1)}, bf16[512,1024]{1,0:T(8,128)(2,1)}, u32[]{:S(2)}) copy-start(bf16[512,1024]{1,0:T(8,128)(2,1)} %constant.14.clone.table_high_ref) | copy-start | bytes 3145732
  34.6 18.4 %copy-start.2 = (bf16[256,1024]{1,0:T(8,128)(2,1)S(1)}, bf16[256,1024]{1,0:T(8,128)(2,1)}, u32[]{:S(2)}) copy-start(bf16[256,1024]{1,0:T(8,128)(2,1)} %constant.17.clone.low_ref) | copy-start | bytes 1572868
  34.6 18.4 %copy-start.3 = (bf16[256,1024]{1,0:T(8,128)(2,1)S(1)}, bf16[256,1024]{1,0:T(8,128)(2,1)}, u32[]{:S(2)}) copy-start(bf16[256,1024]{1,0:T(8,128)(2,1)} %constant.16.clone.high_ref) | copy-start | bytes 1572868

commit v2 on v1

--- a/solution.py
+++ b/solution.py
@@ -25,7 +25,6 @@
 )
 HALO = 2 * SUBSTEPS
 TILE = 8
-GROUPS = 1
 LANES = 128
 F32 = jnp.float32
 BF16 = jnp.bfloat16
@@ -186,58 +185,20 @@
     return out
 
 
-def crystal_kernel(
-    turned_ref, near_ref, far_ref, plate_ref, high_hbm, low_hbm, *rest
-):
-    spots, (third_ref, sent_ref), rest = rest[:4], rest[4:6], rest[6:]
-    kept, (field, trial, angles, result, high_ref, low_ref, sems) = rest[:4], rest[4:]
-    copies = start_copies((high_hbm, low_hbm, *spots), (high_ref, low_ref, *kept), sems)
-    halves, width = turned_ref.shape[1], turned_ref.shape[2]
-    devices = sent_ref.shape[0]
-    index = lax.axis_index("gx")
-    even = lax.rem(index, 2) == 0
-    tiles = width // TILE + 2
-    begin = 2 * TILE
-    keep_first = jnp.where(index > 0, 1.0, 0.0).astype(F32)
-    keep_last = jnp.where(index < devices - 1, 1.0, 0.0).astype(F32)
-
-    zero = jnp.zeros((TILE, LANES), F32)
-    for h in range(halves):
-        for c in range(6):
-            for at in (0, (tiles + 1) * TILE):
-                field[c, h, pl.ds(at, TILE), :] = zero
-                trial[c, h, pl.ds(at, TILE), :] = zero
-        for c in range(4):
-            field[c, h, pl.ds(begin, width), :] = turned_ref[c, h]
-            a, b = near_ref[c, h], far_ref[c, h]
-            field[c, h, pl.ds(TILE, TILE), :] = jnp.where(even, b, a) * keep_first
-            field[c, h, pl.ds(begin + width, TILE), :] = jnp.where(even, a, b) * keep_last
-
-    def store_angles(h, row, value):
-        c1, s1 = sine_pair(value)
-        one = (c1, s1)
-        two = (c1 * c1 - s1 * s1, 2.0 * c1 * s1)
-        three = cmul(one, two)
-        four = (two[0] * two[0] - two[1] * two[1], 2.0 * two[0] * two[1])
-        for z, pair in enumerate((one, two, three, four)):
-            for late in range(2 if z < 3 else 1):
-                at, unit = 4 * z + 2 * late, 0.5 ** (z + late)
-                for k in range(2):
-                    angles[at + k, h, pl.ds(row, TILE), :] = unit * pair[k]
-
-    for h in range(halves):
-        a, b = near_ref[4, h], far_ref[4, h]
-        store_angles(h, TILE, jnp.where(even, b, a))
-        store_angles(h, begin + width, jnp.where(even, a, b))
-
-    def angle_body(t, carry):
-        for h in range(halves):
-            row = pl.multiple_of(t * TILE, TILE)
-            store_angles(h, pl.multiple_of(row + begin, TILE), turned_ref[4, h, pl.ds(row, TILE), :])
-        return carry
-
-    lax.fori_loop(0, width // TILE, angle_body, 0, unroll=2)
-
+def store_angles(angles, h, row, value):
+    c1, s1 = sine_pair(value)
+    one = (c1, s1)
+    two = (c1 * c1 - s1 * s1, 2.0 * c1 * s1)
+    three = cmul(one, two)
+    four = (two[0] * two[0] - two[1] * two[1], 2.0 * two[0] * two[1])
+    for z, pair in enumerate((one, two, three, four)):
+        for late in range(2 if z < 3 else 1):
+            at, unit = 4 * z + 2 * late, 0.5 ** (z + late)
+            for k in range(2):
+                angles[at + k, h, pl.ds(row, TILE), :] = unit * pair[k]
+
+
+def propagate(field, trial, angles, halves, rows, keep, store):
     def turn_at(z, late, row):
         def turn(h):
             if z == 0:
@@ -247,43 +208,104 @@
 
         return turn
 
-    def first_half(step, row, keep):
-        out = advance(field, row, halves, turn_at(step, 1, row), step == 0, range(3))
-        for (c, h), value in out.items():
-            trial[c, h, pl.ds(row, TILE), :] = value if keep is None else value * keep
-
-    def second_half(step, row, keep):
+    for step in range(SUBSTEPS):
         last = step == SUBSTEPS - 1
-        waves = (2,) if last else range(3)
-        out = advance(trial, row, halves, turn_at(step + 1, 0, row), False, waves)
-        for (c, h), value in out.items():
-            if step > 0 or c < 4:
-                value = field[c, h, pl.ds(row, TILE), :] + value
-            if last:
-                at = pl.multiple_of(row - begin, TILE)
-                result[c - 4, h, pl.ds(at, TILE), :] = value * (UNITS[2] * 0.5**SUBSTEPS)
-            else:
-                field[c, h, pl.ds(row, TILE), :] = value if keep is None else value * keep
-
-    def sweep(half, step, edges):
-        count, offset = (tiles, TILE) if edges else (tiles - 2, begin)
-        group = count // GROUPS
-
-        def body(t, carry):
-            for j in range(group):
-                keep = None
-                if edges and j == 0:
-                    keep = jnp.where(t == 0, keep_first, 1.0)
-                elif edges and j == group - 1:
-                    keep = jnp.where(t == GROUPS - 1, keep_last, 1.0)
-                half(step, pl.multiple_of(offset + (t * group + j) * TILE, TILE), keep)
-            return carry
-
-        lax.fori_loop(0, GROUPS, body, 0)
-
-    for step in range(SUBSTEPS):
-        sweep(first_half, step, True)
-        sweep(second_half, step, step < SUBSTEPS - 1)
+        for j, row in enumerate(rows):
+            waves = (2,) if last and j in (0, len(rows) - 1) else range(3)
+            out = advance(field, row, halves, turn_at(step, 1, row), step == 0, waves)
+            for (c, h), value in out.items():
+                trial[c, h, pl.ds(row, TILE), :] = value * keep[j] if j in keep else value
+        for j, row in enumerate(rows[1:-1] if last else rows):
+            waves = (2,) if last else range(3)
+            out = advance(trial, row, halves, turn_at(step + 1, 0, row), False, waves)
+            for (c, h), value in out.items():
+                if step > 0 or c < 4:
+                    value = field[c, h, pl.ds(row, TILE), :] + value
+                if last:
+                    store(c - 4, h, row, value * (UNITS[2] * 0.5**SUBSTEPS))
+                else:
+                    field[c, h, pl.ds(row, TILE), :] = value * keep[j] if j in keep else value
+
+
+def inner_kernel(turned_ref, near_ref, *rest):
+    count = (len(rest) - 5) // 2
+    away_refs, (result_ref, *held_refs) = rest[:count], rest[count : 2 * count + 1]
+    field, trial, angles, sems = rest[2 * count + 1 :]
+    copies = start_copies(away_refs, held_refs, sems)
+    halves, width = turned_ref.shape[1], turned_ref.shape[2]
+    odd = lax.rem(lax.axis_index("gx"), 2)
+    count = width // TILE
+    begin = 2 * TILE
+    first = pl.multiple_of((2 - odd) * TILE, TILE)
+    beside = pl.multiple_of(TILE + (1 - odd) * (width + TILE), TILE)
+
+    zero = jnp.zeros((TILE, LANES), F32)
+    for h in range(halves):
+        for c in range(6):
+            for at in (0, TILE, begin + width, begin + width + TILE):
+                field[c, h, pl.ds(at, TILE), :] = zero
+                trial[c, h, pl.ds(at, TILE), :] = zero
+        for c in range(4):
+            field[c, h, pl.ds(begin, width), :] = turned_ref[c, h]
+            field[c, h, pl.ds(beside, TILE), :] = near_ref[c, h]
+        store_angles(angles, h, beside, near_ref[4, h])
+
+    def angle_body(t, carry):
+        for h in range(halves):
+            row = pl.multiple_of(t * TILE, TILE)
+            value = turned_ref[4, h, pl.ds(row, TILE), :]
+            store_angles(angles, h, pl.multiple_of(row + begin, TILE), value)
+        return carry
+
+    lax.fori_loop(0, count, angle_body, 0, unroll=4)
+    rows = [pl.multiple_of(first + j * TILE, TILE) for j in range(count + 1)]
+
+    def store(p, h, row, value):
+        result_ref[p, h, pl.ds(pl.multiple_of(row - begin, TILE), TILE), :] = value
+
+    propagate(field, trial, angles, halves, rows, {}, store)
+    for copy in copies:
+        copy.wait()
+
+
+def outer_kernel(
+    turned_ref, far_ref, inner_ref, plate_ref, high_ref, low_ref,
+    third_ref, sent_ref,
+    field, trial, angles, result,
+):
+    halves, width = turned_ref.shape[1], turned_ref.shape[2]
+    devices = sent_ref.shape[0]
+    index = lax.axis_index("gx")
+    even = lax.rem(index, 2) == 0
+    present = jnp.where((index > 0) & (index < devices - 1), 1.0, 0.0).astype(F32)
+    keep = {0: jnp.where(even, present, 1.0), 2: jnp.where(even, 1.0, present)}
+    rows = [TILE, 2 * TILE, 3 * TILE]
+
+    zero = jnp.zeros((TILE, LANES), F32)
+    for h in range(halves):
+        for c in range(6):
+            for at in (0, 4 * TILE):
+                field[c, h, pl.ds(at, TILE), :] = zero
+                trial[c, h, pl.ds(at, TILE), :] = zero
+        for c in range(5):
+            beyond = far_ref[c, h]
+            low = [turned_ref[c, h, pl.ds(j * TILE, TILE), :] for j in range(2)]
+            top = [turned_ref[c, h, pl.ds(width - (2 - j) * TILE, TILE), :] for j in range(2)]
+            around = ((beyond, top[0]), (low[0], top[1]), (low[1], beyond))
+            for j, (left, right) in enumerate(around):
+                value = jnp.where(even, left, right)
+                if c < 4:
+                    field[c, h, pl.ds(rows[j], TILE), :] = value * keep[j] if j in keep else value
+                else:
+                    store_angles(angles, h, rows[j], value)
+        for p in range(2):
+            result[p, h] = inner_ref[p, h]
+    edge = pl.multiple_of(jnp.where(even, 0, width - TILE), TILE)
+
+    def store(p, h, row, value):
+        result[p, h, pl.ds(edge, TILE), :] = value
+
+    propagate(field, trial, angles, halves, rows, keep, store)
 
     cosine, sine_part = plate_phase(plate_ref[...])
     parts = [[], []]
@@ -304,8 +326,6 @@
         axis=0,
     )
     high, low = split(data)
-    for copy in copies:
-        copy.wait()
     spectrum = dot(high_ref[...], high) + (dot(high_ref[...], low) + dot(low_ref[...], high))
     share = spectrum.shape[0] // devices
     for d in range(devices):
@@ -314,11 +334,9 @@
 
 
 def spot_kernel(
-    got_ref, third_ref, table_high_ref, table_low_ref, low_ref, high_ref, row_ref, column_ref,
-    far_ref, sent_ref, third_hbm,
-    sems,
+    got_ref, table_high_ref, table_low_ref, low_ref, high_ref, row_ref, column_ref,
+    far_ref, sent_ref,
 ):
-    copies = start_copies((third_ref,), (third_hbm,), sems)
     devices, _, share, width = got_ref.shape
     columns = column_ref.shape[1]
     classes = columns // width
@@ -373,12 +391,14 @@
         k = d % classes
         for p in range(2):
             sent_ref[d, p] = across[p][:, k * width : (k + 1) * width]
-    for copy in copies:
-        copy.wait()
-
-
-def back_kernel(got_ref, far_ref, plate_ref, high_ref, low_ref, back_hbm, far_hbm, back_ref, sems):
-    copies = start_copies((far_ref,), (far_hbm,), sems)
+
+
+def back_kernel(
+    got_ref, far_ref, third_ref, plate_ref, high_ref, low_ref,
+    back_hbm, far_hbm, third_hbm,
+    back_ref, sems,
+):
+    copies = start_copies((far_ref, third_ref), (far_hbm, third_hbm), sems)
     devices, _, share, width = got_ref.shape
     real = got_ref[:, 0].reshape(devices * share, width)
     imaginary = got_ref[:, 1].reshape(devices * share, width)
@@ -399,7 +419,7 @@
         if k % 2:
             done = pl.ds((k - 1) * PLATE, 2 * PLATE)
             copies += start_copies(
-                (back_ref.at[:, done],), (back_hbm.at[:, done],), sems.at[pl.ds(1 + k // 2, 1)]
+                (back_ref.at[:, done],), (back_hbm.at[:, done],), sems.at[pl.ds(2 + k // 2, 1)]
             )
     for copy in copies:
         copy.wait()
@@ -437,7 +457,6 @@
     halves = rows // LANES
     share = far_rows // devices
     assert rows % LANES == 0 and width == LANES and PLATE % halves == 0
-    assert (width // TILE) % GROUPS == 0
     assert far_columns % width == 0 and devices % (far_columns // width) == 0
     assert (whole_width // 2) % far_columns == 0 and devices % 2 == 0
     scale = FAR_SCALE / math.sqrt(rows * whole_width)
@@ -462,40 +481,48 @@
     pairs = [(i, i + 1) for i in range(1, devices - 1, 2)]
     far = lax.ppermute(far, "gx", pairs + [(j, i) for i, j in pairs])
 
-    length = width + 4 * TILE
     spots = [a.reshape(1, -1) for a in (spot_low, spot_high, row_gain, column_gain)]
     chunks = (HELD, shape(devices, 2, share, width))
-    third, sent, *spots = call(
-        crystal_kernel,
-        "crystal",
-        [HELD] * 4 + [AWAY] * 6,
-        [(HELD, whole), chunks, *((HELD, jax.ShapeDtypeStruct(a.shape, a.dtype)) for a in spots)],
-        [
+
+    def planes(length):
+        return [
             pltpu.VMEM((6, halves, length, LANES), F32),
             pltpu.VMEM((6, halves, length, LANES), F32),
             pltpu.VMEM((4 * SUBSTEPS - 2, halves, length, LANES), F32),
-            pltpu.VMEM((2, halves, width, LANES), F32),
-            pltpu.VMEM(forward[0].shape, BF16),
-            pltpu.VMEM(forward[1].shape, BF16),
-            pltpu.SemaphoreType.DMA((6,)),
-        ],
-    )(turned, near, far, plate, *(away(a) for a in (*forward, *spots)))
+        ]
+
+    result = shape(2, halves, width, LANES)
+    fetched = (*forward, *spots)
+    inner, high, low, *spots = call(
+        inner_kernel,
+        "inner",
+        [HELD] * 2 + [AWAY] * len(fetched),
+        [(HELD, result), *((HELD, jax.ShapeDtypeStruct(a.shape, a.dtype)) for a in fetched)],
+        planes(width + 4 * TILE) + [pltpu.SemaphoreType.DMA((len(fetched),))],
+    )(turned, near, *(away(a) for a in fetched))
+    third, sent = call(
+        outer_kernel,
+        "outer",
+        [HELD] * 6,
+        [(HELD, whole), chunks],
+        planes(5 * TILE) + [pltpu.VMEM(result.shape, F32)],
+    )(turned, far, inner, plate, high, low)
     got = lax.all_to_all(sent, "gx", 0, 0, tiled=True)
-    far_field, sent, third = call(
+    far_field, sent = call(
         spot_kernel,
         "spot",
-        [HELD] * 8,
-        [(HELD, shape(2, share, far_columns)), chunks, (AWAY, whole)],
-        [pltpu.SemaphoreType.DMA((1,))],
-    )(got, third, *columns, *spots)
+        [HELD] * 7,
+        [(HELD, shape(2, share, far_columns)), chunks],
+        [],
+    )(got, *columns, *spots)
     got = lax.all_to_all(sent, "gx", 0, 0, tiled=True)
-    back, far_field = call(
+    back, far_field, third = call(
         back_kernel,
         "back",
-        [HELD] * 5,
-        [(AWAY, whole), (AWAY, shape(2, share, far_columns))],
-        [pltpu.VMEM((2, rows, width), F32), pltpu.SemaphoreType.DMA((1 + rows // (2 * PLATE),))],
-    )(got, far_field, plate, *backward)
+        [HELD] * 6,
+        [(AWAY, whole), (AWAY, shape(2, share, far_columns)), (AWAY, whole)],
+        [pltpu.VMEM((2, rows, width), F32), pltpu.SemaphoreType.DMA((2 + rows // (2 * PLATE),))],
+    )(got, far_field, third, plate, *backward)
     return third, far_field, back
 
 

time: 54.5 us -> 52.2 us (0.958)
  blocking collectives: 43.9 us -> 41.1 us
    all_to_all x2, blocking collectives: 43.9 us -> 41.1 us  [local(): got = lax.all_to_all(sent, 'gx', 0, 0, tiled=True)]
    pallas_call x3 -> x4, Pallas kernels: 6.94 us -> 7.36 us  [the longest x1 3.78 us: local(): call(inner_kernel, 'inner', [HELD] * 2 + [AWAY] * len(fetched), [(HELD, r...]
  transfers between devices with their start and end apart: 2 -> 2, of which waited for: 1 -> 1; matrix products, arithmetic and copies ran while one was open for 0% -> 0% of each run, Pallas kernels for 0% -> 7%
where the time goes in v2:
time: 52.2 us; the launch traced here: 52 us
  blocking collectives  41.1 us (79%)
  Pallas kernels  8.71 us (17%)
  starting transfers between devices  1.21 us (2%)
  between operations  0.73 us (1%)
    all_to_all x2, blocking collectives, local(): got = lax.all_to_all(sent, 'gx', 0, 0, tiled=True)  41.1 us
    pallas_call x1, Pallas kernels, local(): call(inner_kernel, 'inner', [HELD] * 2 + [AWAY] * len(fetched), [(HELD, r...  3.78 us
    pallas_call x1, Pallas kernels, local(): call(outer_kernel, 'outer', [HELD] * 6, [(HELD, whole), chunks], planes(5...  1.37 us
    pallas_call x1, Pallas kernels, local(): call(edges_kernel, 'edges', [AWAY] * 3, [(HELD, shape(5, halves, width, L...  1.35 us
    pallas_call x1, Pallas kernels, local(): call(back_kernel, 'back', [HELD] * 6, [(AWAY, whole), (AWAY, shape(2, sha...  1.29 us
  transfers between devices with their start and end apart: 2, of which 1 were waited for; matrix products, arithmetic and copies ran while one was open for 0% of the time, Pallas kernels for 7%

profile of v2, /device:TPU:0, one launch (start us, length us, event | category | flops | bytes accessed | tf_op | source)
XLA Modules:
  0.0 52.0 jit_solution(10601480161314115718)
XLA Ops:
  0.6 1.4 %edges.1 = (f32[5,2,128,128]{3,2,1,0:T(8,128)S(1)}, f32[5,2,8,128]{3,2,1,0:T(8,128)S(1)}, f32[5,2,8,128]{3,2,1,0:T(8,128)S(1)}) custom-call(f32[2,256,128]{2,1,0:T(8,128)} %one_hbm.1, f32[2,256,128]{2,1,0:T(8,128)} %two_hbm.1, f32[256,128]{1,0:T(8,128)} %mismatch_hbm.1), custom_call_target="tpu_custom_call" | custom-call | tf_op jit(solution)/shard_map/edges/pallas_call | solution.py:468
  2.0 0.0 copy-start.4
  2.0 0.6 %collective-permute-start.1 = (f32[5,2,8,128]{3,2,1,0:T(8,128)S(1)}, f32[5,2,8,128]{3,2,1,0:T(8,128)S(1)}, u32[]{:S(2)}, u32[]{:S(2)}) collective-permute-start(f32[5,2,8,128]{3,2,1,0:T(8,128)S(1)} %get-tuple-element.22), channel_id=1, source_target_pairs={{0,1},{1,0},{2,3},{3,2},{4,5},{5,4},{6,7},{7,6},{8,9},{9,8},{10,11... | collective-permute-start | bytes 122888 | tf_op jit(solution)/shard_map/ppermute | solution.py:480
  2.6 0.7 %collective-permute-start = (f32[5,2,8,128]{3,2,1,0:T(8,128)S(1)}, f32[5,2,8,128]{3,2,1,0:T(8,128)S(1)}, u32[]{:S(2)}, u32[]{:S(2)}) collective-permute-start(f32[5,2,8,128]{3,2,1,0:T(8,128)S(1)} %get-tuple-element.21), channel_id=1, source_target_pairs={{1,2},{3,4},{5,6},{7,8},{9,10},{11,12},{13,14},{2,1},{4,3},{6,5},{... | collective-permute-start | bytes 122888 | tf_op jit(solution)/shard_map/ppermute | solution.py:482
  3.2 0.0 copy-done.4
  3.2 0.1 copy.17.plate_ref
  3.3 0.1 collective-permute-done.1.near_ref
  3.4 3.8 %inner.1 = (f32[2,2,128,128]{3,2,1,0:T(8,128)S(1)}, bf16[512,512]{1,0:T(8,128)(2,1)S(1)}, bf16[512,512]{1,0:T(8,128)(2,1)S(1)}, s32[1,512]{1,0:T(1,128)S(1)}, s3...) custom-call(f32[5,2,128,128]{3,2,1,0:T(8,128)S(1)} %get-tuple-element.20.turned_ref, ...), custom_call_target="tpu_custom_call" | custom-call | tf_op jit(solution)/shard_map/inner/pallas_call | solution.py:496
  7.2 0.0 collective-permute-done.far_ref
  7.2 0.0 copy-start
  7.2 0.0 copy-start.1
  7.3 1.4 %outer.1 = (f32[2,256,128]{2,1,0:T(8,128)S(1)}, f32[16,2,32,128]{3,2,1,0:T(8,128)S(1)}) custom-call(f32[5,2,128,128]{3,2,1,0:T(8,128)S(1)} %get-tuple-element.20.turned_ref, f32[5,2,8,128]{3,2,1,0:T(8,128)S(1)} %collective-permute-done.far_ref, f32[2,2,128,128]{3,2,1,0:T(8,128)S(1)} %get-tuple-element.23.inner_ref, s32[8,4]{1,0:T(8,128)S(1)} %copy.17.plate_ref, ...), custom_call_target="tpu_custom_call" | custom-call | tf_op jit(solution)/shard_map/outer/pallas_call | solution.py:503
  8.6 22.7 %all_to_all.10.got_ref = f32[16,2,32,128]{3,2,1,0:T(8,128)S(1)} all-to-all(f32[16,2,32,128]{3,2,1,0:T(8,128)S(1)} %get-tuple-element.26), channel_id=1, replica_groups=mesh['groups'=2,'gx'=16] {'gx'}, dimensions={0} | all-to-all | bytes 1048576 | tf_op jit(solution)/shard_map/all_to_all | solution.py:510
  31.4 0.0 copy-done
  31.4 0.0 copy-done.1
  31.4 0.9 %spot.1 = (f32[2,32,512]{2,1,0:T(8,128)S(1)}, f32[16,2,32,128]{3,2,1,0:T(8,128)S(1)}) custom-call(f32[16,2,32,128]{3,2,1,0:T(8,128)S(1)} %all_to_all.10.got_ref, bf16[512,1024]{1,0:T(8,128)(2,1)S(1)} %copy-done.1, bf16[512,1024]{1,0:T(8,128)(2,1)S(1)} %copy-done, s32[1,512]{1,0:T(1,128)S(1)} %get-tuple-element.27.low_ref, ...), custom_call_target="tpu_custom_call" | custom-call | tf_op jit(solution)/shard_map/spot/pallas_call | solution.py:511
  32.3 0.0 copy-start.2
  32.3 0.0 copy-start.3
  32.3 18.4 %all_to_all.11.got_ref = f32[16,2,32,128]{3,2,1,0:T(8,128)S(1)} all-to-all(f32[16,2,32,128]{3,2,1,0:T(8,128)S(1)} %get-tuple-element.31), channel_id=1, replica_groups=mesh['groups'=2,'gx'=16] {'gx'}, dimensions={0} | all-to-all | bytes 1048576 | tf_op jit(solution)/shard_map/all_to_all | solution.py:518
  50.7 0.0 copy-done.2
  50.7 0.0 copy-done.3
  50.7 1.3 %back.1 = (f32[2,256,128]{2,1,0:T(8,128)}, f32[2,32,512]{2,1,0:T(8,128)}, f32[2,256,128]{2,1,0:T(8,128)}) custom-call(f32[16,2,32,128]{3,2,1,0:T(8,128)S(1)} %all_to_all.11.got_ref, f32[2,32,512]{2,1,0:T(8,128)S(1)} %get-tuple-element.32.far_ref, f32[2,256,128]{2,1,0:T(8,128)S(1)} %get-tuple-element.33.third_ref, s32[8,4]{1,0:T(8,128)S(1)} %copy.17.plate_ref, ...), custom_call_target="tpu_custom_call" | custom-call | tf_op jit(solution)/shard_map/back/pallas_call | solution.py:519
Async XLA Ops:
  2.0 1.2 %copy-start.4 = (s32[8,4]{0,1:T(4,128)S(1)}, s32[8,4]{0,1:T(4,128)}, u32[]{:S(2)}) copy-start(s32[8,4]{0,1:T(4,128)} %param.17) | copy-start | bytes 388
  2.0 1.4 %collective-permute-start.1 = (f32[5,2,8,128]{3,2,1,0:T(8,128)S(1)}, f32[5,2,8,128]{3,2,1,0:T(8,128)S(1)}, u32[]{:S(2)}, u32[]{:S(2)}) collective-permute-start(f32[5,2,8,128]{3,2,1,0:T(8,128)S(1)} %get-tuple-element.22), channel_id=1, source_target_pairs={{0,1},{1,0},{2,3},{3,2},{4,5},{5,4},{6,7},{7,6},{8,9},{9,8},{10,11... | collective-permute-start | bytes 122888 | tf_op jit(solution)/shard_map/ppermute | solution.py:480
  2.6 4.7 %collective-permute-start = (f32[5,2,8,128]{3,2,1,0:T(8,128)S(1)}, f32[5,2,8,128]{3,2,1,0:T(8,128)S(1)}, u32[]{:S(2)}, u32[]{:S(2)}) collective-permute-start(f32[5,2,8,128]{3,2,1,0:T(8,128)S(1)} %get-tuple-element.21), channel_id=1, source_target_pairs={{1,2},{3,4},{5,6},{7,8},{9,10},{11,12},{13,14},{2,1},{4,3},{6,5},{... | collective-permute-start | bytes 122888 | tf_op jit(solution)/shard_map/ppermute | solution.py:482
  7.2 24.1 %copy-start = (bf16[512,1024]{1,0:T(8,128)(2,1)S(1)}, bf16[512,1024]{1,0:T(8,128)(2,1)}, u32[]{:S(2)}) copy-start(bf16[512,1024]{1,0:T(8,128)(2,1)} %constant.15.clone.table_low_ref) | copy-start | bytes 3145732
  7.2 24.1 %copy-start.1 = (bf16[512,1024]{1,0:T(8,128)(2,1)S(1)}, bf16[512,1024]{1,0:T(8,128)(2,1)}, u32[]{:S(2)}) copy-start(bf16[512,1024]{1,0:T(8,128)(2,1)} %constant.14.clone.table_high_ref) | copy-start | bytes 3145732
  32.3 18.4 %copy-start.2 = (bf16[256,1024]{1,0:T(8,128)(2,1)S(1)}, bf16[256,1024]{1,0:T(8,128)(2,1)}, u32[]{:S(2)}) copy-start(bf16[256,1024]{1,0:T(8,128)(2,1)} %constant.17.clone.low_ref) | copy-start | bytes 1572868
  32.3 18.4 %copy-start.3 = (bf16[256,1024]{1,0:T(8,128)(2,1)S(1)}, bf16[256,1024]{1,0:T(8,128)(2,1)}, u32[]{:S(2)}) copy-start(bf16[256,1024]{1,0:T(8,128)(2,1)} %constant.16.clone.high_ref) | copy-start | bytes 1572868

commit v3 on v2

--- a/solution.py
+++ b/solution.py
@@ -67,10 +67,11 @@
 
 def plate_phase(levels):
     count, across = levels.shape
-    block = lax.broadcasted_iota(jnp.int32, (count, across * PLATE), 1) // PLATE
-    level = jnp.zeros((count, across * PLATE), F32)
+    shape = (count, across * PLATE)
+    block = lax.broadcasted_iota(jnp.int32, shape, 1) // PLATE
+    level = jnp.zeros(shape, F32)
     for b in range(across):
-        level = jnp.where(block == b, levels[:, b : b + 1].astype(F32), level)
+        level = jnp.where(block == b, levels[:, b : b + 1], level)
     angle = (2.0 * math.pi / LEVELS) * level
     return jnp.cos(angle), jnp.sin(angle)
 
@@ -85,18 +86,23 @@
 
 
 def edges_kernel(
-    one_hbm, two_hbm, mismatch_hbm, turned_ref, near_ref, far_ref,
-    one_ref, two_ref, mismatch_ref, sems,
+    one_hbm, two_hbm, mismatch_hbm, plate_hbm, turned_ref, near_ref, far_ref, phase_ref,
+    one_ref, two_ref, mismatch_ref, plate_ref, sems,
 ):
     halves = one_ref.shape[1] // LANES
     width = one_ref.shape[2]
     copies = start_copies(
-        (one_hbm, two_hbm, mismatch_hbm), (one_ref, two_ref, mismatch_ref), sems
+        (one_hbm, two_hbm, mismatch_hbm, plate_hbm),
+        (one_ref, two_ref, mismatch_ref, plate_ref),
+        sems,
     )
     even = lax.rem(lax.axis_index("gx"), 2) == 0
     for c in range(5):
         if c % 2 == 0:
             copies[c // 2].wait()
+        if c == 4:
+            copies[3].wait()
+            phase_ref[0], phase_ref[1] = plate_phase(plate_ref[...].astype(F32).T)
         for h in range(halves):
             rows = pl.ds(h, LANES, stride=halves)
             if c < 2:
@@ -114,11 +120,11 @@
 
 def sine_pair(angle):
     q = angle * angle
-    sine = (1.0 / math.factorial(13)) * q - 1.0 / math.factorial(11)
-    cosine = (-1.0 / math.factorial(14)) * q + 1.0 / math.factorial(12)
-    for k in (9, 7, 5, 3, 1):
+    sine = (-1.0 / math.factorial(11)) * q + 1.0 / math.factorial(9)
+    cosine = (1.0 / math.factorial(12)) * q - 1.0 / math.factorial(10)
+    for k in (7, 5, 3, 1):
         sine = sine * q + (-1.0) ** (k // 2) / math.factorial(k)
-    for k in (10, 8, 6, 4, 2, 0):
+    for k in (8, 6, 4, 2, 0):
         cosine = cosine * q + (-1.0) ** (k // 2) / math.factorial(k)
     return cosine, sine * angle
 
@@ -187,15 +193,15 @@
 
 def store_angles(angles, h, row, value):
     c1, s1 = sine_pair(value)
-    one = (c1, s1)
-    two = (c1 * c1 - s1 * s1, 2.0 * c1 * s1)
-    three = cmul(one, two)
-    four = (two[0] * two[0] - two[1] * two[1], 2.0 * two[0] * two[1])
-    for z, pair in enumerate((one, two, three, four)):
-        for late in range(2 if z < 3 else 1):
-            at, unit = 4 * z + 2 * late, 0.5 ** (z + late)
-            for k in range(2):
-                angles[at + k, h, pl.ds(row, TILE), :] = unit * pair[k]
+    one, half = (c1, s1), (0.5 * c1, 0.5 * s1)
+    two = (c1 * half[0] - s1 * half[1], c1 * s1)
+    two_half = (0.5 * two[0], 0.5 * two[1])
+    three = cmul(two, half)
+    three_half = (0.5 * three[0], 0.5 * three[1])
+    four = (two[0] * two_half[0] - two[1] * two_half[1], two[0] * two[1])
+    for at, pair in enumerate((one, half, two, two_half, three, three_half, four)):
+        for k in range(2):
+            angles[2 * at + k, h, pl.ds(row, TILE), :] = pair[k]
 
 
 def propagate(field, trial, angles, halves, rows, keep, store):
@@ -269,7 +275,7 @@
 
 
 def outer_kernel(
-    turned_ref, far_ref, inner_ref, plate_ref, high_ref, low_ref,
+    turned_ref, far_ref, inner_ref, phase_ref, high_ref, low_ref,
     third_ref, sent_ref,
     field, trial, angles, result,
 ):
@@ -307,7 +313,7 @@
 
     propagate(field, trial, angles, halves, rows, keep, store)
 
-    cosine, sine_part = plate_phase(plate_ref[...])
+    cosine, sine_part = phase_ref[0], phase_ref[1]
     parts = [[], []]
     for h in range(halves):
         blocks = [result[p, h].T for p in range(2)]
@@ -394,7 +400,7 @@
 
 
 def back_kernel(
-    got_ref, far_ref, third_ref, plate_ref, high_ref, low_ref,
+    got_ref, far_ref, third_ref, phase_ref, high_ref, low_ref,
     back_hbm, far_hbm, third_hbm,
     back_ref, sems,
 ):
@@ -408,7 +414,7 @@
     )
     high, low = split(data)
     total = dot(high_ref[...], high) + (dot(high_ref[...], low) + dot(low_ref[...], high))
-    cosine, sine_part = plate_phase(plate_ref[...])
+    cosine, sine_part = phase_ref[0], phase_ref[1]
     for k in range(total.shape[0] // PLATE):
         rows = slice(k * PLATE, (k + 1) * PLATE)
         piece = (total[rows, :width], total[rows, width:])
@@ -465,18 +471,24 @@
 
     whole = shape(2, rows, width)
     strip = (HELD, shape(5, halves, HALO, LANES))
-    turned, near, far = call(
+    turned, near, far, phase = call(
         edges_kernel,
         "edges",
-        [AWAY] * 3,
-        [(HELD, shape(5, halves, width, LANES)), strip, strip],
+        [AWAY] * 4,
+        [
+            (HELD, shape(5, halves, width, LANES)),
+            strip,
+            strip,
+            (HELD, shape(2, rows // PLATE, width)),
+        ],
         [
             pltpu.VMEM((2, rows, width), F32),
             pltpu.VMEM((2, rows, width), F32),
             pltpu.VMEM((rows, width), F32),
-            pltpu.SemaphoreType.DMA((3,)),
+            pltpu.VMEM(plate.shape[::-1], plate.dtype),
+            pltpu.SemaphoreType.DMA((4,)),
         ],
-    )(*(away(a) for a in (wave_one, wave_two, mismatch)))
+    )(*(away(a) for a in (wave_one, wave_two, mismatch, plate.T)))
     near = lax.ppermute(near, "gx", [(i, i ^ 1) for i in range(devices)])
     pairs = [(i, i + 1) for i in range(1, devices - 1, 2)]
     far = lax.ppermute(far, "gx", pairs + [(j, i) for i, j in pairs])
@@ -506,7 +518,7 @@
         [HELD] * 6,
         [(HELD, whole), chunks],
         planes(5 * TILE) + [pltpu.VMEM(result.shape, F32)],
-    )(turned, far, inner, plate, high, low)
+    )(turned, far, inner, phase, high, low)
     got = lax.all_to_all(sent, "gx", 0, 0, tiled=True)
     far_field, sent = call(
         spot_kernel,
@@ -522,7 +534,7 @@
         [HELD] * 6,
         [(AWAY, whole), (AWAY, shape(2, share, far_columns)), (AWAY, whole)],
         [pltpu.VMEM((2, rows, width), F32), pltpu.SemaphoreType.DMA((2 + rows // (2 * PLATE),))],
-    )(got, far_field, third, plate, *backward)
+    )(got, far_field, third, phase, *backward)
     return third, far_field, back
 
 

time: 52.2 us -> 52.2 us (level)
  no operation moved by 1% of the time
where the time goes in v3:
time: 52.2 us; the launch traced here: 51.9 us
  blocking collectives  41 us (79%)
  Pallas kernels  8.75 us (17%)
  starting transfers between devices  1.21 us (2%)
  between operations  0.71 us (1%)
    all_to_all x2, blocking collectives, local(): got = lax.all_to_all(sent, 'gx', 0, 0, tiled=True)  41 us
    pallas_call x1, Pallas kernels, local(): call(inner_kernel, 'inner', [HELD] * 2 + [AWAY] * len(fetched), [(HELD, r...  3.74 us
    pallas_call x1, Pallas kernels, local(): call(edges_kernel, 'edges', [AWAY] * 4, [(HELD, shape(5, halves, width, L...  1.46 us
    pallas_call x1, Pallas kernels, local(): call(outer_kernel, 'outer', [HELD] * 6, [(HELD, whole), chunks], planes(5...  1.34 us
    pallas_call x1, Pallas kernels, local(): call(back_kernel, 'back', [HELD] * 6, [(AWAY, whole), (AWAY, shape(2, sha...  1.29 us
  transfers between devices with their start and end apart: 2, of which 1 were waited for; matrix products, arithmetic and copies ran while one was open for 0% of the time, Pallas kernels for 7%

profile of v3, /device:TPU:0, one launch (start us, length us, event | category | flops | bytes accessed | tf_op | source)
XLA Modules:
  0.0 51.9 jit_solution(1326876641737603146)
XLA Ops:
  0.6 1.5 %edges.1 = (f32[5,2,128,128]{3,2,1,0:T(8,128)S(1)}, f32[5,2,8,128]{3,2,1,0:T(8,128)S(1)}, f32[5,2,8,128]{3,2,1,0:T(8,128)S(1)}, f32[2,8,128]{2,1,0:T(8,128)S(1)}) custom-call(f32[2,256,128]{2,1,0:T(8,128)} %one_hbm.1, f32[2,256,128]{2,1,0:T(8,128)} %two_hbm.1, f32[256,128]{1,0:T(8,128)} %mismatch_hbm.1, s32[4,8]{1,0:T(4,128)} %bitcast.5), custom_call_target="tpu_custom_call" | custom-call | tf_op jit(solution)/shard_map/edges/pallas_call | solution.py:474
  2.1 0.6 %collective-permute-start.1 = (f32[5,2,8,128]{3,2,1,0:T(8,128)S(1)}, f32[5,2,8,128]{3,2,1,0:T(8,128)S(1)}, u32[]{:S(2)}, u32[]{:S(2)}) collective-permute-start(f32[5,2,8,128]{3,2,1,0:T(8,128)S(1)} %get-tuple-element.23), channel_id=1, source_target_pairs={{0,1},{1,0},{2,3},{3,2},{4,5},{5,4},{6,7},{7,6},{8,9},{9,8},{10,11... | collective-permute-start | bytes 122888 | tf_op jit(solution)/shard_map/ppermute | solution.py:492
  2.7 0.7 %collective-permute-start = (f32[5,2,8,128]{3,2,1,0:T(8,128)S(1)}, f32[5,2,8,128]{3,2,1,0:T(8,128)S(1)}, u32[]{:S(2)}, u32[]{:S(2)}) collective-permute-start(f32[5,2,8,128]{3,2,1,0:T(8,128)S(1)} %get-tuple-element.22), channel_id=1, source_target_pairs={{1,2},{3,4},{5,6},{7,8},{9,10},{11,12},{13,14},{2,1},{4,3},{6,5},{... | collective-permute-start | bytes 122888 | tf_op jit(solution)/shard_map/ppermute | solution.py:494
  3.3 0.2 collective-permute-done.1.near_ref
  3.5 3.7 %inner.1 = (f32[2,2,128,128]{3,2,1,0:T(8,128)S(1)}, bf16[512,512]{1,0:T(8,128)(2,1)S(1)}, bf16[512,512]{1,0:T(8,128)(2,1)S(1)}, s32[1,512]{1,0:T(1,128)S(1)}, s3...) custom-call(f32[5,2,128,128]{3,2,1,0:T(8,128)S(1)} %get-tuple-element.21.turned_ref, ...), custom_call_target="tpu_custom_call" | custom-call | tf_op jit(solution)/shard_map/inner/pallas_call | solution.py:508
  7.3 0.0 collective-permute-done.far_ref
  7.3 0.0 copy-start
  7.3 0.0 copy-start.1
  7.3 1.3 %outer.1 = (f32[2,256,128]{2,1,0:T(8,128)S(1)}, f32[16,2,32,128]{3,2,1,0:T(8,128)S(1)}) custom-call(f32[5,2,128,128]{3,2,1,0:T(8,128)S(1)} %get-tuple-element.21.turned_ref, f32[5,2,8,128]{3,2,1,0:T(8,128)S(1)} %collective-permute-done.far_ref, f32[2,2,128,128]{3,2,1,0:T(8,128)S(1)} %get-tuple-element.24.inner_ref, ...), custom_call_target="tpu_custom_call" | custom-call | tf_op jit(solution)/shard_map/outer/pallas_call | solution.py:515
  8.7 22.7 %all_to_all.10.got_ref = f32[16,2,32,128]{3,2,1,0:T(8,128)S(1)} all-to-all(f32[16,2,32,128]{3,2,1,0:T(8,128)S(1)} %get-tuple-element.28), channel_id=1, replica_groups=mesh['groups'=2,'gx'=16] {'gx'}, dimensions={0} | all-to-all | bytes 1048576 | tf_op jit(solution)/shard_map/all_to_all | solution.py:522
  31.3 0.0 copy-done
  31.3 0.0 copy-done.1
  31.3 0.9 %spot.1 = (f32[2,32,512]{2,1,0:T(8,128)S(1)}, f32[16,2,32,128]{3,2,1,0:T(8,128)S(1)}) custom-call(f32[16,2,32,128]{3,2,1,0:T(8,128)S(1)} %all_to_all.10.got_ref, bf16[512,1024]{1,0:T(8,128)(2,1)S(1)} %copy-done.1, bf16[512,1024]{1,0:T(8,128)(2,1)S(1)} %copy-done, s32[1,512]{1,0:T(1,128)S(1)} %get-tuple-element.29.low_ref, ...), custom_call_target="tpu_custom_call" | custom-call | tf_op jit(solution)/shard_map/spot/pallas_call | solution.py:523
  32.3 0.0 copy-start.2
  32.3 0.0 copy-start.3
  32.3 18.4 %all_to_all.11.got_ref = f32[16,2,32,128]{3,2,1,0:T(8,128)S(1)} all-to-all(f32[16,2,32,128]{3,2,1,0:T(8,128)S(1)} %get-tuple-element.33), channel_id=1, replica_groups=mesh['groups'=2,'gx'=16] {'gx'}, dimensions={0} | all-to-all | bytes 1048576 | tf_op jit(solution)/shard_map/all_to_all | solution.py:530
  50.6 0.0 copy-done.2
  50.7 0.0 copy-done.3
  50.7 1.3 %back.1 = (f32[2,256,128]{2,1,0:T(8,128)}, f32[2,32,512]{2,1,0:T(8,128)}, f32[2,256,128]{2,1,0:T(8,128)}) custom-call(f32[16,2,32,128]{3,2,1,0:T(8,128)S(1)} %all_to_all.11.got_ref, f32[2,32,512]{2,1,0:T(8,128)S(1)} %get-tuple-element.34.far_ref, f32[2,256,128]{2,1,0:T(8,128)S(1)} %get-tuple-element.35.third_ref, ...), custom_call_target="tpu_custom_call" | custom-call | tf_op jit(solution)/shard_map/back/pallas_call | solution.py:531
Async XLA Ops:
  2.1 1.4 %collective-permute-start.1 = (f32[5,2,8,128]{3,2,1,0:T(8,128)S(1)}, f32[5,2,8,128]{3,2,1,0:T(8,128)S(1)}, u32[]{:S(2)}, u32[]{:S(2)}) collective-permute-start(f32[5,2,8,128]{3,2,1,0:T(8,128)S(1)} %get-tuple-element.23), channel_id=1, source_target_pairs={{0,1},{1,0},{2,3},{3,2},{4,5},{5,4},{6,7},{7,6},{8,9},{9,8},{10,11... | collective-permute-start | bytes 122888 | tf_op jit(solution)/shard_map/ppermute | solution.py:492
  2.7 4.6 %collective-permute-start = (f32[5,2,8,128]{3,2,1,0:T(8,128)S(1)}, f32[5,2,8,128]{3,2,1,0:T(8,128)S(1)}, u32[]{:S(2)}, u32[]{:S(2)}) collective-permute-start(f32[5,2,8,128]{3,2,1,0:T(8,128)S(1)} %get-tuple-element.22), channel_id=1, source_target_pairs={{1,2},{3,4},{5,6},{7,8},{9,10},{11,12},{13,14},{2,1},{4,3},{6,5},{... | collective-permute-start | bytes 122888 | tf_op jit(solution)/shard_map/ppermute | solution.py:494
  7.3 24.0 %copy-start = (bf16[512,1024]{1,0:T(8,128)(2,1)S(1)}, bf16[512,1024]{1,0:T(8,128)(2,1)}, u32[]{:S(2)}) copy-start(bf16[512,1024]{1,0:T(8,128)(2,1)} %constant.15.clone.table_low_ref) | copy-start | bytes 3145732
  7.3 24.0 %copy-start.1 = (bf16[512,1024]{1,0:T(8,128)(2,1)S(1)}, bf16[512,1024]{1,0:T(8,128)(2,1)}, u32[]{:S(2)}) copy-start(bf16[512,1024]{1,0:T(8,128)(2,1)} %constant.14.clone.table_high_ref) | copy-start | bytes 3145732
  32.3 18.4 %copy-start.2 = (bf16[256,1024]{1,0:T(8,128)(2,1)S(1)}, bf16[256,1024]{1,0:T(8,128)(2,1)}, u32[]{:S(2)}) copy-start(bf16[256,1024]{1,0:T(8,128)(2,1)} %constant.17.clone.low_ref) | copy-start | bytes 1572868
  32.3 18.4 %copy-start.3 = (bf16[256,1024]{1,0:T(8,128)(2,1)S(1)}, bf16[256,1024]{1,0:T(8,128)(2,1)}, u32[]{:S(2)}) copy-start(bf16[256,1024]{1,0:T(8,128)(2,1)} %constant.16.clone.high_ref) | copy-start | bytes 1572868
